TPU v7x, 32 devices: a whole 2x2x4 slice. The times are simulated.
32 devices in a mesh: dp: 8 (over y, x, core), mp: 4 (over z).
Axes of the slice: x: 2, y: 2, z: 4, core: 2. Of those that a mesh axis runs over, the one named last changes fastest.
Arguments:
- tokens: bfloat16 [16384, 1024], P(('dp', 'mp')), may hold values from -6 to 6
- norm_gain: float32 [2, 1024], replicated, may hold values from 0.1 to 1.9
- qkv_weight: bfloat16 [3, 1024, 1024], P(None, 'dp', 'mp')
- out_weight: bfloat16 [1024, 1024], P('mp', 'dp'), may hold values from -0.1875 to 0.1875
- variate_bias: float32 [2, 16], replicated, may hold values from -6 to 6
- ffn_weight: bfloat16 [2, 1024, 2816], P(None, 'dp', 'mp'), may hold values from -0.1875 to 0.1875
- down_weight: bfloat16 [2816, 1024], P('mp', 'dp'), may hold values from -0.109375 to 0.109375
- sample_ids: int32 [16384], P(('dp', 'mp')), may hold values from 0 to 127, as said below
- variate_ids: int32 [16384], P(('dp', 'mp')), may hold values from 0 to 15, as said below
- time_ids: int32 [16384], P(('dp', 'mp')), may hold values from 0 to 31, as said below
Outputs:
- encoded: bfloat16 [16384, 1024], P(('dp', 'mp'))
Inputs may be any that keep to these rules, and one draw needn't show every extreme that they name: `sample_ids`: within each packed sequence of 512 tokens the series numbers start at 0 and never fall; a series with v variates (1 to 16) and p patches (4 to 32) holds v * p consecutive tokens, the last series of a sequence may be cut short; some packed sequence holds 128 series of one variate and four patches each. `variate_ids`: A token's offset within its series divided by that series' patch count p. `time_ids`: A token's offset within its series modulo that series' patch count p.
All inputs are finite; a program needn't handle non-finite values.
Results may differ from a plain program's by a relative error of at most 0.017.
Values may be sent and summed in bfloat16 or wider, within the bound.
A program may use at most 128 MiB of HBM per device.

v0:
```python
import jax
import jax.numpy as jnp
from jax import lax
from jax.sharding import PartitionSpec as P

HEAD_DIM = 64
L = 512


def rms_norm(values, gain):
    wide = values.astype(jnp.float32)
    square = jnp.mean(wide * wide, axis=-1, keepdims=True)
    return (wide * lax.rsqrt(square + 1e-05) * gain[None, :]).astype(jnp.bfloat16)


def rotate(values, times):
    half = values.shape[-1] // 2
    freq = 10000.0 ** (-jnp.arange(half, dtype=jnp.float32) / half)
    angle = times.astype(jnp.float32)[:, None] * freq[None, :]
    cosine = jnp.cos(angle)[:, None, :]
    sine = jnp.sin(angle)[:, None, :]
    first = values[..., :half]
    second = values[..., half:]
    return jnp.concatenate(
        [first * cosine - second * sine, first * sine + second * cosine], axis=-1
    )


def rotated(raw, times):
    row_total, local_width = raw.shape
    turned = rotate(raw.reshape(row_total, local_width // HEAD_DIM, HEAD_DIM), times)
    return turned.reshape(row_total, local_width).astype(jnp.bfloat16)


def attend(queries, keys_rot, values, samples, variates, bias):
    row_total, local_width = queries.shape
    heads_here = local_width // HEAD_DIM
    count = row_total // L

    def one_sequence(args):
        qs, ks, vs, sample_row, variate_row = args
        scores = jnp.einsum(
            "qhd,khd->hqk", qs, ks, preferred_element_type=jnp.float32
        ) * HEAD_DIM ** (-0.5)
        same = variate_row[:, None] == variate_row[None, :]
        scores = scores + jnp.where(same[None], bias[0][:, None, None], bias[1][:, None, None])
        scores = jnp.where((sample_row[:, None] == sample_row[None, :])[None], scores, -1e30)
        top = jnp.max(scores, axis=2, keepdims=True)
        expo = jnp.exp(scores - top)
        weights = (expo / jnp.sum(expo, axis=2, keepdims=True)).astype(jnp.bfloat16)
        return jnp.einsum("hqk,khd->qhd", weights, vs, preferred_element_type=jnp.float32).astype(
            jnp.bfloat16
        )

    shape = (count, L, heads_here, HEAD_DIM)
    result = lax.map(
        one_sequence,
        (
            queries.reshape(shape),
            keys_rot.reshape(shape),
            values.reshape(shape),
            samples.reshape(count, L),
            variates.reshape(count, L),
        ),
    )
    return result.reshape(row_total, local_width)


def local(
    tokens,
    norm_gain,
    qkv_weight,
    out_weight,
    variate_bias,
    ffn_weight,
    down_weight,
    sample_ids,
    variate_ids,
    time_ids,
):
    heads_here = qkv_weight.shape[2] // HEAD_DIM
    head_start = lax.axis_index("mp") * heads_here
    bias_local = lax.dynamic_slice_in_dim(variate_bias, head_start, heads_here, 1)
    first_normed = rms_norm(tokens, norm_gain[0])
    wide_columns = lax.all_gather(qkv_weight, "mp", axis=2, tiled=True)
    columns = first_normed
    projected = jnp.einsum(
        "rc,jcd->jrd",
        columns,
        lax.all_gather(wide_columns, "dp", axis=1, tiled=True),
        preferred_element_type=jnp.float32,
    )
    queries = rotated(projected[0], time_ids)
    keys_rot = rotated(projected[1], time_ids)
    values = projected[2].astype(jnp.bfloat16)
    grouped = lax.all_to_all(
        jnp.stack([queries, keys_rot, values]), "mp", split_axis=2, concat_axis=1, tiled=True
    )
    gathered_ids = (
        lax.all_gather(sample_ids, "mp", axis=0, tiled=True),
        lax.all_gather(variate_ids, "mp", axis=0, tiled=True),
    )
    attended = attend(
        grouped[0], grouped[1], grouped[2], gathered_ids[0], gathered_ids[1], bias_local
    )
    back_rows = lax.all_to_all(attended, "mp", split_axis=0, concat_axis=1, tiled=True)
    out_rows = lax.all_gather(out_weight, "mp", axis=0, tiled=True)
    mixed = jnp.dot(
        back_rows,
        lax.all_gather(out_rows, "dp", axis=1, tiled=True),
        preferred_element_type=jnp.float32,
    )
    residual = (tokens.astype(jnp.float32) + mixed).astype(jnp.bfloat16)
    second_normed = rms_norm(residual, norm_gain[1])
    ffn_columns = lax.all_gather(ffn_weight, "mp", axis=2, tiled=True)
    columns = second_normed
    gate_up = jnp.einsum(
        "rc,jcf->jrf",
        columns,
        lax.all_gather(ffn_columns, "dp", axis=1, tiled=True),
        preferred_element_type=jnp.float32,
    )
    hidden = (jax.nn.silu(gate_up[0]) * gate_up[1]).astype(jnp.bfloat16)
    down_full = lax.all_gather(down_weight, "mp", axis=0, tiled=True)
    feed = jnp.dot(
        hidden,
        lax.all_gather(down_full, "dp", axis=1, tiled=True),
        preferred_element_type=jnp.float32,
    )
    return (residual.astype(jnp.float32) + feed).astype(jnp.bfloat16)


def solution(mesh):
    return jax.shard_map(
        local,
        mesh=mesh,
        in_specs=(
            P(("dp", "mp"), None),
            P(),
            P(None, "dp", "mp"),
            P("mp", "dp"),
            P(),
            P(None, "dp", "mp"),
            P("mp", "dp"),
            P(("dp", "mp")),
            P(("dp", "mp")),
            P(("dp", "mp")),
        ),
        out_specs=P(("dp", "mp"), None),
        check_vma=False,
    )
```

profile of v0, /device:TPU:0, one launch (start us, length us, event | category | flops | bytes accessed | tf_op | source)
XLA Modules:
  0.0 358.3 jit_solution(14907393396261247635)
XLA Ops:
  6.5 2.2 copy.40
  8.8 27.7 %all_gather.30 = bf16[3,128,1024]{2,1,0:T(8,128)(2,1)} all-gather(bf16[3,128,256]{2,1,0:T(8,128)(2,1)} %param.14), channel_id=1, replica_groups=mesh['dp'=8,'mp'=4] {'mp'}, dimensions={2}, use_global_device_ids=true | all-gather | bytes 983040 | tf_op jit(solution)/shard_map/all_gather | solution.py:85
  36.6 18.9 %all_gather.34 = bf16[1024,128]{1,0:T(8,128)(2,1)} all-gather(bf16[256,128]{1,0:T(8,128)(2,1)} %param.15), channel_id=1, replica_groups=mesh['dp'=8,'mp'=4] {'mp'}, dimensions={0}, use_global_device_ids=true | all-gather | bytes 327680 | tf_op jit(solution)/shard_map/all_gather | solution.py:107
  55.5 1.2 all-gather.12.cloned.1.call-done
  56.8 4.9 %copy.41 = bf16[2,128,2816]{2,1,0:T(8,128)(2,1)} copy(bf16[2,128,2816]{1,0,2:T(2,128)(2,1)} %all-gather.12.cloned.1.call-done) | data formatting | bytes 2883584 | tf_op jit(solution)/shard_map/all_gather | solution.py:115
  61.7 0.3 fusion.56
  62.0 0.3 multiply_cosine_fusion
  62.3 41.2 %all-gather.8.cloned.1.call-done = bf16[3,1024,1024]{2,1,0:T(8,128)(2,1)} async-done(((bf16[3,128,1024]{2,1,0:T(8,128)(2,1)}), bf16[3,1024,1024]{2,1,0:T(8,128)(2,1)}) %all-gather.8.cloned.1.call-update) | async-done | bytes 6291472 | tf_op jit(solution)/shard_map/all_gather | solution.py:90
  103.5 5.7 %convolution_bitcast_fusion.1 = f32[3,512,1024]{2,1,0:T(8,128)S(1)} fusion(bf16[3,1024,1024]{2,1,0:T(8,128)(2,1)} %all-gather.8.cloned.1.call-done, bf16[512,1024]{1,0:T(8,128)(2,1)S(1)} %copy-done.2, f32[1024]{0:T(1024)S(1)} %bitcast.128, f32[512]{0:T(512)S(1)} %add_rsqrt_fusion.1), kind=kOutput, calls=%fused_computation.54 | convolution fusion | flops 3223322624 | bytes 13637632 | tf_op jit(solution)/shard_map/rc,jcd->jrd/dot_general | solution.py:87
  109.3 1.1 slice.103
  110.4 2.4 fusion.80
  112.8 2.0 copy.34
  114.8 2.9 copy.35
  117.7 2.3 subtract_convert_fusion.1
  120.0 0.1 pad_maximum_fusion.1
  120.1 1.3 copy.36
  121.5 1.3 copy.37
  122.8 2.5 pad_maximum_fusion
  125.3 5.7 %copy.38 = bf16[3,512,1024]{1,0,2:T(4,128)(2,1)} copy(bf16[3,512,1024]{2,1,0:T(8,128)(2,1)S(1)} %pad_maximum_fusion) | data formatting | bytes 6291456 | tf_op jit(solution)/shard_map/stack | solution.py:97
  131.0 5.0 %all-to-all-start = ((bf16[3,512,1024]{1,0,2:T(4,128)(2,1)}), bf16[3,512,1024]{1,0,2:T(4,128)(2,1)}, u32[]{:S(2)}, u32[]{:S(2)}) async-start(bf16[3,512,1024]{1,0,2:T(4,128)(2,1)} %copy.38), calls=%async_computation | async-start | bytes 8388608 | tf_op jit(solution)/shard_map/all_to_all | solution.py:96
  136.1 106.7 %all_gather.38 = bf16[2816,128]{1,0:T(8,128)(2,1)} all-gather(bf16[704,128]{1,0:T(8,128)(2,1)S(1)} %copy-done.4), channel_id=1, replica_groups=mesh['dp'=8,'mp'=4] {'mp'}, dimensions={0}, use_global_device_ids=true | all-gather | bytes 901120 | tf_op jit(solution)/shard_map/all_gather | solution.py:124
  242.9 11.9 %all-gather.1 = s32[4,1,512]{2,1,0:T(1,128)S(1)} all-gather(s32[1,1,512]{2,1,0:T(1,128)S(1)} %bitcast.129), channel_id=1, replica_groups=mesh['dp'=8,'mp'=4] {'mp'}, dimensions={0}, use_global_device_ids=true | all-gather | bytes 10240 | tf_op jit(solution)/shard_map/all_gather | solution.py:101
  254.8 12.1 %all-gather = s32[4,1,512]{2,1,0:T(1,128)S(1)} all-gather(s32[1,1,512]{2,1,0:T(1,128)S(1)} %bitcast.130), channel_id=1, replica_groups=mesh['dp'=8,'mp'=4] {'mp'}, dimensions={0}, use_global_device_ids=true | all-gather | bytes 10240 | tf_op jit(solution)/shard_map/all_gather | solution.py:100
  266.9 0.1 constant_dynamic-slice_fusion.2
  267.0 3.2 copy.39
  270.2 1.5 fusion.81
  271.7 31.2 %while.10 = (s32[]{:T(128)}, bf16[4,512,4,64]{1,3,2,0:T(8,128)(2,1)}, bf16[4,512,4,64]{1,3,2,0:T(8,128)(2,1)}, s32[4,512]{1,0:T(4,128)S(1)}, bf16[4,512,4,64]{1,...) while((s32[]{:T(128)}, ...), condition=%wide.region_4.5_spmd, body=%wide.region_1.4_spmd.sunk | while | flops 416943104 | bytes 3179681 | solution.py:56
  271.7 0.2 broadcast_compare_fusion.4
  271.9 0.2 broadcast_compare_fusion.5
  272.2 3.0 fusion.100
  275.2 4.3 %fusion.101 = bf16[4,512,4,64]{1,3,2,0:T(8,128)(2,1)} fusion(bf16[4,512,4,64]{1,3,2,0:T(8,128)(2,1)} %get-tuple-element.154, s32[]{:T(128)} %get-tuple-element.153, f32[4,512]{1,0:T(4,128)S(1)} %fusion.100, bf16[4,512,4,64]{1,3,2,0:T(8,128)(2,1)} %get-tuple-element.164, f32[4]{0:T(128)S(1)} %get-tuple-element.140, f32[4]{0:T(128)S(1)} %get-tuple-element.141, ...), kind=kOutput, calls=%fused_computation.14.clone.1 | convolution fusion | flops 275909120 | bytes 1584128 | tf_op jit(solution)/shard_map/while/body/eval_jaxpr/hqk,khd->qhd/dot_general | solution.py:51
  279.5 0.2 broadcast_compare_fusion.4
  279.7 0.2 broadcast_compare_fusion.5
  280.0 3.0 fusion.100
  283.0 4.3 %fusion.101 = bf16[4,512,4,64]{1,3,2,0:T(8,128)(2,1)} fusion(bf16[4,512,4,64]{1,3,2,0:T(8,128)(2,1)} %get-tuple-element.154, s32[]{:T(128)} %get-tuple-element.153, f32[4,512]{1,0:T(4,128)S(1)} %fusion.100, bf16[4,512,4,64]{1,3,2,0:T(8,128)(2,1)} %get-tuple-element.164, f32[4]{0:T(128)S(1)} %get-tuple-element.140, f32[4]{0:T(128)S(1)} %get-tuple-element.141, ...), kind=kOutput, calls=%fused_computation.14.clone.1 | convolution fusion | flops 275909120 | bytes 1584128 | tf_op jit(solution)/shard_map/while/body/eval_jaxpr/hqk,khd->qhd/dot_general | solution.py:51
  287.3 0.2 broadcast_compare_fusion.4
  287.5 0.2 broadcast_compare_fusion.5
  287.8 3.0 fusion.100
  290.8 4.3 %fusion.101 = bf16[4,512,4,64]{1,3,2,0:T(8,128)(2,1)} fusion(bf16[4,512,4,64]{1,3,2,0:T(8,128)(2,1)} %get-tuple-element.154, s32[]{:T(128)} %get-tuple-element.153, f32[4,512]{1,0:T(4,128)S(1)} %fusion.100, bf16[4,512,4,64]{1,3,2,0:T(8,128)(2,1)} %get-tuple-element.164, f32[4]{0:T(128)S(1)} %get-tuple-element.140, f32[4]{0:T(128)S(1)} %get-tuple-element.141, ...), kind=kOutput, calls=%fused_computation.14.clone.1 | convolution fusion | flops 275909120 | bytes 1584128 | tf_op jit(solution)/shard_map/while/body/eval_jaxpr/hqk,khd->qhd/dot_general | solution.py:51
  295.1 0.2 broadcast_compare_fusion.4
  295.4 0.2 broadcast_compare_fusion.5
  295.6 3.0 fusion.100
  298.6 4.3 %fusion.101 = bf16[4,512,4,64]{1,3,2,0:T(8,128)(2,1)} fusion(bf16[4,512,4,64]{1,3,2,0:T(8,128)(2,1)} %get-tuple-element.154, s32[]{:T(128)} %get-tuple-element.153, f32[4,512]{1,0:T(4,128)S(1)} %fusion.100, bf16[4,512,4,64]{1,3,2,0:T(8,128)(2,1)} %get-tuple-element.164, f32[4]{0:T(128)S(1)} %get-tuple-element.140, f32[4]{0:T(128)S(1)} %get-tuple-element.141, ...), kind=kOutput, calls=%fused_computation.14.clone.1 | convolution fusion | flops 275909120 | bytes 1584128 | tf_op jit(solution)/shard_map/while/body/eval_jaxpr/hqk,khd->qhd/dot_general | solution.py:51
  302.9 3.7 %all-to-all-start.1 = ((bf16[4,512,256]{1,2,0:T(8,128)(2,1)}), bf16[4,512,256]{1,2,0:T(8,128)(2,1)S(1)}, u32[]{:S(2)}, u32[]{:S(2)}) async-start(bf16[4,512,256]{1,2,0:T(8,128)(2,1)} %bitcast.24), calls=%async_computation.1 | async-start | bytes 2097152 | tf_op jit(solution)/shard_map/all_to_all | solution.py:106
  306.7 18.6 %all-to-all-done.1 = bf16[4,512,256]{1,2,0:T(8,128)(2,1)S(1)} async-done(((bf16[4,512,256]{1,2,0:T(8,128)(2,1)}), bf16[4,512,256]{1,2,0:T(8,128)(2,1)S(1)}, u32[]{:S(2)}, u32[]{:S(2)}) %all-to-all-start.1) | async-done | bytes 1048608 | tf_op jit(solution)/shard_map/all_to_all | solution.py:106
  325.3 3.0 fusion.60
  328.3 13.2 %convolution_bitcast_fusion = f32[2,512,2816]{2,1,0:T(8,128)} fusion(bf16[2,1024,2816]{2,1,0:T(8,128)(2,1)} %all-gather.14.cloned.1.call-done, bf16[512,1024]{1,0:T(8,128)(2,1)S(1)} %get-tuple-element.84, f32[1024]{0:T(1024)S(1)} %bitcast.125, f32[512]{0:T(512)S(1)} %add_rsqrt_fusion), kind=kOutput, calls=%fused_computation.41 | convolution fusion | flops 5907677184 | bytes 24123392 | tf_op jit(solution)/shard_map/rc,jcf->jrf/dot_general | solution.py:117
  341.6 10.2 %fusion.63 = bf16[512,1024]{1,0:T(8,128)(2,1)} fusion(bf16[512,1024]{1,0:T(8,128)(2,1)S(1)} %get-tuple-element.84, bf16[2816,1024]{1,0:T(8,128)(2,1)} %all-gather.16.cloned.1.call-done, f32[2,512,2816]{2,1,0:T(8,128)} %convolution_bitcast_fusion), kind=kOutput, calls=%fused_computation.62 | convolution fusion | flops 2963013632 | bytes 19398656 | tf_op jit(solution)/shard_map/dot_general | solution.py:125
  (48 shorter events, 0.4 us)
Async XLA Ops:
  6.5 260.4 %copy-start = (f32[2,16]{1,0:T(2,128)S(1)}, f32[2,16]{1,0:T(2,128)}, u32[]{:S(2)}) copy-start(f32[2,16]{1,0:T(2,128)} %param.16) | copy-start | bytes 388
  6.5 55.1 %copy-start.8 = (s32[512]{0:T(512)S(1)}, s32[512]{0:T(512)}, u32[]{:S(2)}) copy-start(s32[512]{0:T(512)} %param.21) | copy-start | bytes 6148
  6.5 55.2 %copy-start.2 = (bf16[512,1024]{1,0:T(8,128)(2,1)S(1)}, bf16[512,1024]{1,0:T(8,128)(2,1)}, u32[]{:S(2)}) copy-start(bf16[512,1024]{1,0:T(8,128)(2,1)} %param.12) | copy-start | bytes 3145732
  6.5 50.2 %all-gather.12.cloned.1.call-start = ((), (), s32[]{:S(2)}) async-start(), calls=%async_computation.4 | async-start | bytes 1802240 | tf_op jit(solution)/shard_map/all_gather | solution.py:115
  8.7 53.3 %copy-start.5 = (f32[2,1024]{1,0:T(2,128)S(1)}, f32[2,1024]{1,0:T(2,128)}, u32[]{:S(2)}) copy-start(f32[2,1024]{1,0:T(2,128)} %param.13) | copy-start | bytes 24580
  8.8 94.8 %all-gather.8.cloned.1.call-start = ((), (), s32[]{:S(2)}) async-start(), calls=%async_computation.2 | async-start | bytes 7077888 | tf_op jit(solution)/shard_map/all_gather | solution.py:90
  36.5 270.2 %all-gather.10.cloned.1.call-start = ((), (), s32[]{:S(2)}) async-start(), calls=%async_computation.3 | async-start | bytes 2359296 | tf_op jit(solution)/shard_map/all_gather | solution.py:110
  55.5 272.8 %all-gather.14.cloned.1.call-start = ((), (), s32[]{:S(2)}) async-start(), calls=%async_computation.5 | async-start | bytes 12976128 | tf_op jit(solution)/shard_map/all_gather | solution.py:120
  131.0 5.1 %copy-start.4 = (bf16[704,128]{1,0:T(8,128)(2,1)S(1)}, bf16[704,128]{1,0:T(8,128)(2,1)}, u32[]{:S(2)}) copy-start(bf16[704,128]{1,0:T(8,128)(2,1)} %param.18) | copy-start | bytes 540676
  131.0 111.8 %copy-start.6 = (s32[512]{0:T(512)S(1)}, s32[512]{0:T(512)}, u32[]{:S(2)}) copy-start(s32[512]{0:T(512)} %param.20) | copy-start | bytes 6148
  131.0 123.8 %copy-start.7 = (s32[512]{0:T(512)S(1)}, s32[512]{0:T(512)}, u32[]{:S(2)}) copy-start(s32[512]{0:T(512)} %param.19) | copy-start | bytes 6148
  131.0 136.0 %all-to-all-start = ((bf16[3,512,1024]{1,0,2:T(4,128)(2,1)}), bf16[3,512,1024]{1,0,2:T(4,128)(2,1)}, u32[]{:S(2)}, u32[]{:S(2)}) async-start(bf16[3,512,1024]{1,0,2:T(4,128)(2,1)} %copy.38), calls=%async_computation | async-start | bytes 8388608 | tf_op jit(solution)/shard_map/all_to_all | solution.py:96
  136.0 205.6 %all-gather.16.cloned.1.call-start = ((), (), s32[]{:S(2)}) async-start(), calls=%async_computation.6 | async-start | bytes 6488064 | tf_op jit(solution)/shard_map/all_gather | solution.py:127
  271.7 53.6 %copy-start.3 = (bf16[512,1024]{1,0:T(8,128)(2,1)S(1)}, bf16[512,1024]{1,0:T(8,128)(2,1)}, u32[]{:S(2)}) copy-start(bf16[512,1024]{1,0:T(8,128)(2,1)} %param.12) | copy-start | bytes 3145732
  302.9 22.3 %all-to-all-start.1 = ((bf16[4,512,256]{1,2,0:T(8,128)(2,1)}), bf16[4,512,256]{1,2,0:T(8,128)(2,1)S(1)}, u32[]{:S(2)}, u32[]{:S(2)}) async-start(bf16[4,512,256]{1,2,0:T(8,128)(2,1)} %bitcast.24), calls=%async_computation.1 | async-start | bytes 2097152 | tf_op jit(solution)/shard_map/all_to_all | solution.py:106
  341.6 10.2 %copy-start.1 = (f32[2,16]{1,0:T(2,128)S(1)}, f32[2,16]{1,0:T(2,128)}, u32[]{:S(2)}) copy-start(f32[2,16]{1,0:T(2,128)} %param.16) | copy-start | bytes 388
Sparse Core Ops, SparseCore 0:
  8.9 47.8 all-gather.11
  58.7 44.7 all-gather.7
  105.4 28.0 all-gather.9
  135.3 67.5 all-gather.13
  243.0 44.4 all-gather.15
where the time goes:
time: 359 us; the launch traced here: 358 us
  blocking collectives  177 us (49%)
  matrix products  61.5 us (17%)
  waiting for transfers between devices  61.1 us (17%)
  local copies, waits for them, and re-layouts  28.7 us (8%)
  between operations  13.3 us (4%)
  starting transfers between devices  8.9 us (2%)
  other arithmetic  7.24 us (2%)
    all_gather x1, blocking collectives, local(): down_full = lax.all_gather(down_weight, 'mp', axis=0, tiled=True)  107 us
    all_gather x1, waiting for transfers between devices, local(): lax.all_gather(wide_columns, 'dp', axis=1, tiled=True)  41.2 us
    all_gather x1, blocking collectives, local(): wide_columns = lax.all_gather(qkv_weight, 'mp', axis=2, tiled=True)  27.7 us
    all_gather x1, blocking collectives, local(): out_rows = lax.all_gather(out_weight, 'mp', axis=0, tiled=True)  18.9 us
    all_to_all x1, waiting for transfers between devices, local(): lax.all_to_all(attended, 'mp', split_axis=0, concat_axis=1, tiled=True)  18.6 us
    dot_general x4, matrix products, one_sequence(): jnp.einsum('hqk,khd->qhd', weights, vs, preferred_element_type=jnp.float32)  17.2 us
    dot_general x1, matrix products, local(): jnp.einsum('rc,jcf->jrf', columns, lax.all_gather(ffn_columns, 'dp', axis...  13.2 us
    sub x4, matrix products, one_sequence(): expo = jnp.exp(scores - top)  12.1 us
  transfers between devices with their start and end apart: 7, of which 3 were waited for; matrix products, arithmetic and copies ran while one was open for 24% of the time, Pallas kernels for 0%

commit v1 on v0

--- a/solution.py
+++ b/solution.py
@@ -82,7 +82,12 @@
     head_start = lax.axis_index("mp") * heads_here
     bias_local = lax.dynamic_slice_in_dim(variate_bias, head_start, heads_here, 1)
     first_normed = rms_norm(tokens, norm_gain[0])
-    wide_columns = lax.all_gather(qkv_weight, "mp", axis=2, tiled=True)
+    ring = [qkv_weight]
+    for hop in range(3):
+        ring.append(lax.ppermute(ring[-1], "mp", [(dev, (dev + 1) % 4) for dev in range(4)]))
+    wide_columns = jnp.roll(
+        jnp.concatenate(ring[::-1], axis=2), (lax.axis_index("mp") + 1) * ring[0].shape[2], axis=2
+    )
     columns = first_normed
     projected = jnp.einsum(
         "rc,jcd->jrd",

time: 359 us -> 344 us (0.958)
  blocking collectives: 177 us -> 149 us
  waiting for transfers between devices: 61.1 us -> 84.1 us
  local copies, waits for them, and re-layouts: 28.7 us -> 19.4 us
  other arithmetic: 7.24 us -> 3.55 us
    ppermute x0 -> x3, waiting for transfers between devices: none -> 33 us  [local(): lax.ppermute(ring[-1], 'mp', [(dev, (dev + 1) % 4) for dev in range(4)])]
    all_gather x1 -> x0, blocking collectives: 27.7 us -> none  [local(): wide_columns = lax.all_gather(qkv_weight, 'mp', axis=2, tiled=True)]
    all_gather x1, waiting for transfers between devices: 41.2 us -> 32.2 us  [local(): lax.all_gather(wide_columns, 'dp', axis=1, tiled=True)]
    slice x2 -> x1, local copies, waits for them, and re-layouts: 4.39 us -> 0.44 us  [local(): queries = rotated(projected[0], time_ids)]
  transfers between devices with their start and end apart: 7 -> 10, of which waited for: 3 -> 5; matrix products, arithmetic and copies ran while one was open for 24% -> 21% of each run, Pallas kernels for 0% -> 0%
where the time goes in v1:
time: 344 us; the launch traced here: 343 us
  blocking collectives  149 us (43%)
  waiting for transfers between devices  84.1 us (24%)
  matrix products  61.6 us (18%)
  local copies, waits for them, and re-layouts  19.4 us (6%)
  between operations  13.4 us (4%)
  starting transfers between devices  11.8 us (3%)
  other arithmetic  3.55 us (1%)
    all_gather x1, blocking collectives, local(): down_full = lax.all_gather(down_weight, 'mp', axis=0, tiled=True)  107 us
    ppermute x3, waiting for transfers between devices, local(): lax.ppermute(ring[-1], 'mp', [(dev, (dev + 1) % 4) for dev in range(4)])  33 us
    all_gather x1, waiting for transfers between devices, local(): lax.all_gather(wide_columns, 'dp', axis=1, tiled=True)  32.2 us
    all_to_all x1, waiting for transfers between devices, local(): lax.all_to_all(attended, 'mp', split_axis=0, concat_axis=1, tiled=True)  18.8 us
    all_gather x1, blocking collectives, local(): out_rows = lax.all_gather(out_weight, 'mp', axis=0, tiled=True)  18.2 us
    dot_general x4, matrix products, one_sequence(): jnp.einsum('hqk,khd->qhd', weights, vs, preferred_element_type=jnp.float32)  17.2 us
    dot_general x1, matrix products, local(): jnp.einsum('rc,jcf->jrf', columns, lax.all_gather(ffn_columns, 'dp', axis...  13.2 us
    sub x4, matrix products, one_sequence(): expo = jnp.exp(scores - top)  12.1 us
  transfers between devices with their start and end apart: 10, of which 5 were waited for; matrix products, arithmetic and copies ran while one was open for 21% of the time, Pallas kernels for 0%

profile of v1, /device:TPU:0, one launch (start us, length us, event | category | flops | bytes accessed | tf_op | source)
XLA Modules:
  0.0 343.0 jit_solution(10446594139064830189)
XLA Ops:
  6.5 2.1 copy.29
  8.7 1.1 copy.24
  9.8 3.1 collective-permute-start
  12.9 6.9 %collective-permute-done = bf16[3,128,256]{1,2,0:T(8,128)(2,1)S(1)} collective-permute-done((bf16[3,128,256]{1,2,0:T(8,128)(2,1)S(1)}, bf16[3,128,256]{1,2,0:T(8,128)(2,1)S(1)}, u32[]{:S(2)}, u32[]{:S(2)}) %collective-permute-start) | collective-permute-done | bytes 196640 | tf_op jit(solution)/shard_map/ppermute | solution.py:87
  19.9 13.0 %collective-permute-done.1 = bf16[3,128,256]{1,2,0:T(8,128)(2,1)S(1)} collective-permute-done((bf16[3,128,256]{1,2,0:T(8,128)(2,1)S(1)}, bf16[3,128,256]{1,2,0:T(8,128)(2,1)S(1)}, u32[]{:S(2)}, u32[]{:S(2)}) %collective-permute-start.1) | collective-permute-done | bytes 196640 | tf_op jit(solution)/shard_map/ppermute | solution.py:87
  32.9 13.0 %collective-permute-done.2 = bf16[3,128,256]{1,2,0:T(8,128)(2,1)S(1)} collective-permute-done((bf16[3,128,256]{1,2,0:T(8,128)(2,1)S(1)}, bf16[3,128,256]{1,2,0:T(8,128)(2,1)S(1)}, u32[]{:S(2)}, u32[]{:S(2)}) %collective-permute-start.2) | collective-permute-done | bytes 196640 | tf_op jit(solution)/shard_map/ppermute | solution.py:87
  46.2 0.9 constant_dynamic-slice_fusion.3
  47.2 18.2 %all_gather.30 = bf16[1024,128]{1,0:T(8,128)(2,1)} all-gather(bf16[256,128]{1,0:T(8,128)(2,1)S(1)} %copy-done.4), channel_id=1, replica_groups=mesh['dp'=8,'mp'=4] {'mp'}, dimensions={0}, use_global_device_ids=true | all-gather | bytes 327680 | tf_op jit(solution)/shard_map/all_gather | solution.py:112
  65.6 5.0 %copy.30 = bf16[2,128,2816]{2,1,0:T(8,128)(2,1)} copy(bf16[2,128,2816]{1,0,2:T(2,128)(2,1)} %all-gather.12.cloned.1.call-done) | data formatting | bytes 2883584 | tf_op jit(solution)/shard_map/all_gather | solution.py:120
  70.6 0.3 fusion.56
  70.9 0.3 multiply_cosine_fusion
  71.2 32.2 %all-gather.8.cloned.1.call-done = bf16[3,1024,1024]{1,2,0:T(8,128)(2,1)} async-done(((bf16[3,128,1024]{1,2,0:T(8,128)(2,1)}), bf16[3,1024,1024]{1,2,0:T(8,128)(2,1)}) %all-gather.8.cloned.1.call-update) | async-done | bytes 6291472 | tf_op jit(solution)/shard_map/all_gather | solution.py:95
  103.4 5.8 %convolution_bitcast_fusion.1 = f32[3,512,1024]{1,2,0:T(8,128)S(1)} fusion(bf16[3,1024,1024]{1,2,0:T(8,128)(2,1)} %all-gather.8.cloned.1.call-done, bf16[512,1024]{1,0:T(8,128)(2,1)S(1)} %copy-done.2, f32[1024]{0:T(1024)S(1)} %bitcast.128, f32[512]{0:T(512)S(1)} %add_rsqrt_fusion.1), kind=kOutput, calls=%fused_computation.54 | convolution fusion | flops 3223322624 | bytes 13637632 | tf_op jit(solution)/shard_map/rc,jcd->jrd/dot_general | solution.py:92
  109.2 0.1 slice.103
  109.3 0.4 fusion.80
  109.8 0.7 subtract_convert_fusion.1
  110.5 0.1 pad_maximum_fusion.1
  110.7 0.3 pad_maximum_fusion
  111.0 4.6 %copy.27 = bf16[3,512,1024]{1,0,2:T(4,128)(2,1)} copy(bf16[3,512,1024]{1,2,0:T(8,128)(2,1)S(1)} %pad_maximum_fusion) | data formatting | bytes 6291456 | tf_op jit(solution)/shard_map/stack | solution.py:102
  115.7 5.0 %all-to-all-start = ((bf16[3,512,1024]{1,0,2:T(4,128)(2,1)}), bf16[3,512,1024]{1,0,2:T(4,128)(2,1)}, u32[]{:S(2)}, u32[]{:S(2)}) async-start(bf16[3,512,1024]{1,0,2:T(4,128)(2,1)} %copy.27), calls=%async_computation | async-start | bytes 8388608 | tf_op jit(solution)/shard_map/all_to_all | solution.py:101
  120.7 106.7 %all_gather.34 = bf16[2816,128]{1,0:T(8,128)(2,1)} all-gather(bf16[704,128]{1,0:T(8,128)(2,1)S(1)} %copy-done.3), channel_id=1, replica_groups=mesh['dp'=8,'mp'=4] {'mp'}, dimensions={0}, use_global_device_ids=true | all-gather | bytes 901120 | tf_op jit(solution)/shard_map/all_gather | solution.py:129
  227.5 11.9 %all-gather.1 = s32[4,1,512]{2,1,0:T(1,128)S(1)} all-gather(s32[1,1,512]{2,1,0:T(1,128)S(1)} %bitcast.129), channel_id=1, replica_groups=mesh['dp'=8,'mp'=4] {'mp'}, dimensions={0}, use_global_device_ids=true | all-gather | bytes 10240 | tf_op jit(solution)/shard_map/all_gather | solution.py:106
  239.5 12.1 %all-gather = s32[4,1,512]{2,1,0:T(1,128)S(1)} all-gather(s32[1,1,512]{2,1,0:T(1,128)S(1)} %bitcast.130), channel_id=1, replica_groups=mesh['dp'=8,'mp'=4] {'mp'}, dimensions={0}, use_global_device_ids=true | all-gather | bytes 10240 | tf_op jit(solution)/shard_map/all_gather | solution.py:105
  251.6 0.1 constant_dynamic-slice_fusion.2
  251.6 3.2 copy.28
  254.8 1.6 fusion.81
  256.4 31.2 %while.10 = (s32[]{:T(128)}, bf16[4,512,4,64]{1,3,2,0:T(8,128)(2,1)}, bf16[4,512,4,64]{1,3,2,0:T(8,128)(2,1)}, s32[4,512]{1,0:T(4,128)S(1)}, bf16[4,512,4,64]{1,...) while((s32[]{:T(128)}, ...), condition=%wide.region_4.5_spmd, body=%wide.region_1.4_spmd.sunk | while | flops 416943104 | bytes 3179681 | solution.py:56
  256.4 0.2 broadcast_compare_fusion.4
  256.6 0.2 broadcast_compare_fusion.5
  256.8 3.0 fusion.100
  259.9 4.3 %fusion.101 = bf16[4,512,4,64]{1,3,2,0:T(8,128)(2,1)} fusion(bf16[4,512,4,64]{1,3,2,0:T(8,128)(2,1)} %get-tuple-element.154, s32[]{:T(128)} %get-tuple-element.153, f32[4,512]{1,0:T(4,128)S(1)} %fusion.100, bf16[4,512,4,64]{1,3,2,0:T(8,128)(2,1)} %get-tuple-element.164, f32[4]{0:T(128)S(1)} %get-tuple-element.140, f32[4]{0:T(128)S(1)} %get-tuple-element.141, ...), kind=kOutput, calls=%fused_computation.14.clone.1 | convolution fusion | flops 275909120 | bytes 1584128 | tf_op jit(solution)/shard_map/while/body/eval_jaxpr/hqk,khd->qhd/dot_general | solution.py:51
  264.2 0.2 broadcast_compare_fusion.4
  264.4 0.2 broadcast_compare_fusion.5
  264.6 3.0 fusion.100
  267.7 4.3 %fusion.101 = bf16[4,512,4,64]{1,3,2,0:T(8,128)(2,1)} fusion(bf16[4,512,4,64]{1,3,2,0:T(8,128)(2,1)} %get-tuple-element.154, s32[]{:T(128)} %get-tuple-element.153, f32[4,512]{1,0:T(4,128)S(1)} %fusion.100, bf16[4,512,4,64]{1,3,2,0:T(8,128)(2,1)} %get-tuple-element.164, f32[4]{0:T(128)S(1)} %get-tuple-element.140, f32[4]{0:T(128)S(1)} %get-tuple-element.141, ...), kind=kOutput, calls=%fused_computation.14.clone.1 | convolution fusion | flops 275909120 | bytes 1584128 | tf_op jit(solution)/shard_map/while/body/eval_jaxpr/hqk,khd->qhd/dot_general | solution.py:51
  272.0 0.2 broadcast_compare_fusion.4
  272.2 0.2 broadcast_compare_fusion.5
  272.4 3.0 fusion.100
  275.5 4.3 %fusion.101 = bf16[4,512,4,64]{1,3,2,0:T(8,128)(2,1)} fusion(bf16[4,512,4,64]{1,3,2,0:T(8,128)(2,1)} %get-tuple-element.154, s32[]{:T(128)} %get-tuple-element.153, f32[4,512]{1,0:T(4,128)S(1)} %fusion.100, bf16[4,512,4,64]{1,3,2,0:T(8,128)(2,1)} %get-tuple-element.164, f32[4]{0:T(128)S(1)} %get-tuple-element.140, f32[4]{0:T(128)S(1)} %get-tuple-element.141, ...), kind=kOutput, calls=%fused_computation.14.clone.1 | convolution fusion | flops 275909120 | bytes 1584128 | tf_op jit(solution)/shard_map/while/body/eval_jaxpr/hqk,khd->qhd/dot_general | solution.py:51
  279.8 0.2 broadcast_compare_fusion.4
  280.0 0.2 broadcast_compare_fusion.5
  280.2 3.0 fusion.100
  283.3 4.3 %fusion.101 = bf16[4,512,4,64]{1,3,2,0:T(8,128)(2,1)} fusion(bf16[4,512,4,64]{1,3,2,0:T(8,128)(2,1)} %get-tuple-element.154, s32[]{:T(128)} %get-tuple-element.153, f32[4,512]{1,0:T(4,128)S(1)} %fusion.100, bf16[4,512,4,64]{1,3,2,0:T(8,128)(2,1)} %get-tuple-element.164, f32[4]{0:T(128)S(1)} %get-tuple-element.140, f32[4]{0:T(128)S(1)} %get-tuple-element.141, ...), kind=kOutput, calls=%fused_computation.14.clone.1 | convolution fusion | flops 275909120 | bytes 1584128 | tf_op jit(solution)/shard_map/while/body/eval_jaxpr/hqk,khd->qhd/dot_general | solution.py:51
  287.6 3.5 %all-to-all-start.1 = ((bf16[4,512,256]{1,2,0:T(8,128)(2,1)}), bf16[4,512,256]{1,2,0:T(8,128)(2,1)S(1)}, u32[]{:S(2)}, u32[]{:S(2)}) async-start(bf16[4,512,256]{1,2,0:T(8,128)(2,1)} %bitcast.24), calls=%async_computation.1 | async-start | bytes 2097152 | tf_op jit(solution)/shard_map/all_to_all | solution.py:111
  291.1 18.8 %all-to-all-done.1 = bf16[4,512,256]{1,2,0:T(8,128)(2,1)S(1)} async-done(((bf16[4,512,256]{1,2,0:T(8,128)(2,1)}), bf16[4,512,256]{1,2,0:T(8,128)(2,1)S(1)}, u32[]{:S(2)}, u32[]{:S(2)}) %all-to-all-start.1) | async-done | bytes 1048608 | tf_op jit(solution)/shard_map/all_to_all | solution.py:111
  309.9 3.0 fusion.60
  313.0 13.2 %convolution_bitcast_fusion = f32[2,512,2816]{2,1,0:T(8,128)} fusion(bf16[2,1024,2816]{2,1,0:T(8,128)(2,1)} %all-gather.14.cloned.1.call-done, bf16[512,1024]{1,0:T(8,128)(2,1)S(1)} %get-tuple-element.84, f32[1024]{0:T(1024)S(1)} %bitcast.125, f32[512]{0:T(512)S(1)} %add_rsqrt_fusion), kind=kOutput, calls=%fused_computation.41 | convolution fusion | flops 5907677184 | bytes 24123392 | tf_op jit(solution)/shard_map/rc,jcf->jrf/dot_general | solution.py:122
  326.2 10.2 %fusion.63 = bf16[512,1024]{1,0:T(8,128)(2,1)} fusion(bf16[512,1024]{1,0:T(8,128)(2,1)S(1)} %get-tuple-element.84, bf16[2816,1024]{1,0:T(8,128)(2,1)} %all-gather.16.cloned.1.call-done, f32[2,512,2816]{2,1,0:T(8,128)} %convolution_bitcast_fusion), kind=kOutput, calls=%fused_computation.62 | convolution fusion | flops 2963013632 | bytes 19398656 | tf_op jit(solution)/shard_map/dot_general | solution.py:130
  (59 shorter events, 0.7 us)
Async XLA Ops:
  6.5 245.0 %copy-start = (f32[2,16]{1,0:T(2,128)S(1)}, f32[2,16]{1,0:T(2,128)}, u32[]{:S(2)}) copy-start(f32[2,16]{1,0:T(2,128)} %param.16) | copy-start | bytes 388
  6.5 59.0 %all-gather.12.cloned.1.call-start = ((), (), s32[]{:S(2)}) async-start(), calls=%async_computation.4 | async-start | bytes 1802240 | tf_op jit(solution)/shard_map/all_gather | solution.py:120
  8.7 38.5 %copy-start.4 = (bf16[256,128]{1,0:T(8,128)(2,1)S(1)}, bf16[256,128]{1,0:T(8,128)(2,1)}, u32[]{:S(2)}) copy-start(bf16[256,128]{1,0:T(8,128)(2,1)} %param.15) | copy-start | bytes 196612
  8.7 94.7 %all-gather.8.cloned.1.call-start = ((), (), s32[]{:S(2)}) async-start(), calls=%async_computation.2 | async-start | bytes 7077888 | tf_op jit(solution)/shard_map/all_gather | solution.py:95
  9.8 10.0 %collective-permute-start = (bf16[3,128,256]{1,2,0:T(8,128)(2,1)S(1)}, bf16[3,128,256]{1,2,0:T(8,128)(2,1)S(1)}, u32[]{:S(2)}, u32[]{:S(2)}) collective-permute-start(bf16[3,128,256]{1,2,0:T(8,128)(2,1)S(1)} %copy.24), channel_id=1, source_target_pairs={{0,1},{1,2},{2,3},{3,0},{4,5},{5,6},{6,7},{7,4},{8,9},{9,10},{10,1... | collective-permute-start | bytes 589832 | tf_op jit(solution)/shard_map/ppermute | solution.py:87
  19.9 13.0 %collective-permute-start.1 = (bf16[3,128,256]{1,2,0:T(8,128)(2,1)S(1)}, bf16[3,128,256]{1,2,0:T(8,128)(2,1)S(1)}, u32[]{:S(2)}, u32[]{:S(2)}) collective-permute-start(bf16[3,128,256]{1,2,0:T(8,128)(2,1)S(1)} %collective-permute-done), channel_id=1, source_target_pairs={{0,1},{1,2},{2,3},{3,0},{4,5},{5,6},{6,7},{7,4},{8,9},{9,10},{10,1... | collective-permute-start | bytes 589832 | tf_op jit(solution)/shard_map/ppermute | solution.py:87
  32.9 13.0 %collective-permute-start.2 = (bf16[3,128,256]{1,2,0:T(8,128)(2,1)S(1)}, bf16[3,128,256]{1,2,0:T(8,128)(2,1)S(1)}, u32[]{:S(2)}, u32[]{:S(2)}) collective-permute-start(bf16[3,128,256]{1,2,0:T(8,128)(2,1)S(1)} %collective-permute-done.1), channel_id=1, source_target_pairs={{0,1},{1,2},{2,3},{3,0},{4,5},{5,6},{6,7},{7,4},{8,9},{9,10},{10,1... | collective-permute-start | bytes 589832 | tf_op jit(solution)/shard_map/ppermute | solution.py:87
  47.1 23.4 %copy-start.8 = (s32[512]{0:T(512)S(1)}, s32[512]{0:T(512)}, u32[]{:S(2)}) copy-start(s32[512]{0:T(512)} %param.21) | copy-start | bytes 6148
  47.1 23.5 %copy-start.2 = (bf16[512,1024]{1,0:T(8,128)(2,1)S(1)}, bf16[512,1024]{1,0:T(8,128)(2,1)}, u32[]{:S(2)}) copy-start(bf16[512,1024]{1,0:T(8,128)(2,1)} %param.12) | copy-start | bytes 3145732
  47.2 244.0 %all-gather.10.cloned.1.call-start = ((), (), s32[]{:S(2)}) async-start(), calls=%async_computation.3 | async-start | bytes 2359296 | tf_op jit(solution)/shard_map/all_gather | solution.py:115
  65.4 5.4 %copy-start.5 = (f32[2,1024]{1,0:T(2,128)S(1)}, f32[2,1024]{1,0:T(2,128)}, u32[]{:S(2)}) copy-start(f32[2,1024]{1,0:T(2,128)} %param.13) | copy-start | bytes 24580
  65.5 247.5 %all-gather.14.cloned.1.call-start = ((), (), s32[]{:S(2)}) async-start(), calls=%async_computation.5 | async-start | bytes 12976128 | tf_op jit(solution)/shard_map/all_gather | solution.py:125
  115.7 5.1 %copy-start.3 = (bf16[704,128]{1,0:T(8,128)(2,1)S(1)}, bf16[704,128]{1,0:T(8,128)(2,1)}, u32[]{:S(2)}) copy-start(bf16[704,128]{1,0:T(8,128)(2,1)} %param.18) | copy-start | bytes 540676
  115.7 111.8 %copy-start.6 = (s32[512]{0:T(512)S(1)}, s32[512]{0:T(512)}, u32[]{:S(2)}) copy-start(s32[512]{0:T(512)} %param.20) | copy-start | bytes 6148
  115.7 123.8 %copy-start.7 = (s32[512]{0:T(512)S(1)}, s32[512]{0:T(512)}, u32[]{:S(2)}) copy-start(s32[512]{0:T(512)} %param.19) | copy-start | bytes 6148
  115.7 136.0 %all-to-all-start = ((bf16[3,512,1024]{1,0,2:T(4,128)(2,1)}), bf16[3,512,1024]{1,0,2:T(4,128)(2,1)}, u32[]{:S(2)}, u32[]{:S(2)}) async-start(bf16[3,512,1024]{1,0,2:T(4,128)(2,1)} %copy.27), calls=%async_computation | async-start | bytes 8388608 | tf_op jit(solution)/shard_map/all_to_all | solution.py:101
  120.7 205.6 %all-gather.16.cloned.1.call-start = ((), (), s32[]{:S(2)}) async-start(), calls=%async_computation.6 | async-start | bytes 6488064 | tf_op jit(solution)/shard_map/all_gather | solution.py:132
  287.6 22.4 %all-to-all-start.1 = ((bf16[4,512,256]{1,2,0:T(8,128)(2,1)}), bf16[4,512,256]{1,2,0:T(8,128)(2,1)S(1)}, u32[]{:S(2)}, u32[]{:S(2)}) async-start(bf16[4,512,256]{1,2,0:T(8,128)(2,1)} %bitcast.24), calls=%async_computation.1 | async-start | bytes 2097152 | tf_op jit(solution)/shard_map/all_to_all | solution.py:111
  326.2 10.2 %copy-start.1 = (f32[2,16]{1,0:T(2,128)S(1)}, f32[2,16]{1,0:T(2,128)}, u32[]{:S(2)}) copy-start(f32[2,16]{1,0:T(2,128)} %param.16) | copy-start | bytes 388
Sparse Core Ops, SparseCore 0:
  8.9 47.4 all-gather.11
  58.3 45.0 all-gather.7
  105.3 28.0 all-gather.9
  135.2 67.5 all-gather.13
  227.6 44.5 all-gather.15
